TPU v7x, 256 devices: a whole 4x4x8 slice. The times are simulated.
256 devices in a mesh: src: 8 (over x, y_hi), rcv: 32 (over y_lo, z, core).
Axes of the slice: x: 4, y: 4 (y_hi: 2, y_lo: 2; y = y_hi * 2 + y_lo), z: 8, core: 2. Of those that a mesh axis runs over, the one named last changes fastest.
Arguments:
- wavefield: float32 [2, 16, 2048, 2048], P(None, None, 'rcv', 'src')
- surface_band: float32 [2, 2048, 1024], P(None, 'rcv'), may hold values from -0.75 to 0.75
- band_shift: int32 [32], P('rcv'), may hold values from -16 to 16
- trace_mask: int32 [2048], P('rcv'), may hold values 0 or 1
- shot_taper: float32 [5], replicated, may hold values from 0.2 to 1
Outputs:
- multiples: float32 [2, 16, 2048, 2048], P(None, None, 'rcv', 'src')
- primaries: float32 [2, 16, 2048, 2048], P(None, None, 'rcv', 'src')
All inputs are finite; a program needn't handle non-finite values. No bound on the sum of `trace_mask` on one device may be relied on, other than what follows from the above.
Results may differ from a plain program's by a relative error of at most 0.0003.
Values sent between devices are 32-bit elements; how exact they have to be, the bound alone decides.
A program may use at most 64 MiB of HBM per device.

v0:
```python
import functools

import jax
import jax.numpy as jnp
from jax import lax
from jax.sharding import Mesh
from jax.sharding import PartitionSpec as P

APER = 64
SHIFT = 16
BLOCK = 64
SHALF = 2
RCV = ("rcv_0", "rcv_1", "rcv_2")
SRC = ("src_0", "src_1")
SRC_RCV = ("src_0", "src_1", "rcv_0", "rcv_1", "rcv_2")


def extended(cells, sides, width):
    for axis, dim in sides:
        count = lax.axis_size(axis)
        ends = count - 1
        head = lax.slice_in_dim(cells, 0, width, axis=dim)
        tail = lax.slice_in_dim(cells, cells.shape[dim] - width, cells.shape[dim], axis=dim)
        cells = jnp.concatenate(
            [
                lax.ppermute(tail, axis, [(i, (i + 1) % count) for i in range(ends)]),
                cells,
                lax.ppermute(head, axis, [((i + 1) % count, i) for i in range(ends)]),
            ],
            axis=dim,
        )
    return cells


def by_axis(array, axes):
    return functools.reduce(lax.psum, axes, array)


def band_matrix(band_piece):
    columns = band_piece.shape[3]
    taps = band_piece.shape[2]
    rows_index = jnp.arange(columns + taps - 1, dtype=jnp.int32)
    cols_index = jnp.arange(columns, dtype=jnp.int32)
    tap_index = jnp.arange(taps, dtype=jnp.int32)
    onehot = (
        tap_index[:, None, None] == rows_index[None, :, None] - cols_index[None, None, :]
    ).astype(jnp.float32)
    return jnp.einsum("xftc,tjc->xfjc", band_piece, onehot, precision=lax.Precision.HIGHEST)


def complex_product(window, band):
    real_part = jnp.einsum(
        "fjc,fjs->fcs", band[0], window[0], precision=lax.Precision.HIGHEST
    ) - jnp.einsum("fjc,fjs->fcs", band[1], window[1], precision=lax.Precision.HIGHEST)
    imag_part = jnp.einsum(
        "fjc,fjs->fcs", band[1], window[0], precision=lax.Precision.HIGHEST
    ) + jnp.einsum("fjc,fjs->fcs", band[0], window[1], precision=lax.Precision.HIGHEST)
    return jnp.stack([real_part, imag_part])


def receiver_products(padded, band_local, band_shift, halo_width):
    start = halo_width - APER // 2 + band_shift[0]
    window = lax.dynamic_slice_in_dim(padded, start, BLOCK + APER - 1, 2)
    outputs = complex_product(window, band_matrix(band_local))
    return outputs


def taper_rows(padded, shot_taper, shots):
    result = shot_taper[0] * padded[:, :, :, 0:shots]
    for offset_row in range(1, 2 * SHALF + 1):
        result = result + shot_taper[offset_row] * padded[:, :, :, offset_row : offset_row + shots]
    return result


def per_device(wavefield, surface_band, band_shift, trace_mask, shot_taper):
    shots = wavefield.shape[3]
    slices = wavefield.shape[1]
    receivers = wavefield.shape[2]
    band_local = jnp.transpose(surface_band.reshape(2, receivers, slices, APER), (0, 2, 3, 1))
    masked = wavefield * trace_mask.astype(jnp.float32)[None, None, :, None]
    halo_width = APER // 2 + SHIFT
    padded = extended(masked, ((RCV, 2),), halo_width)
    predicted = receiver_products(padded, band_local, band_shift, halo_width)
    shot_padded = extended(predicted, ((SRC, 3),), SHALF)
    multiples = taper_rows(shot_padded, shot_taper, shots)
    data_energy = jnp.sum(wavefield * wavefield, axis=(0, 2, 3))
    pred_energy = jnp.sum(multiples * multiples, axis=(0, 2, 3))
    data_energy, pred_energy = (by_axis(data_energy, SRC_RCV), by_axis(pred_energy, SRC_RCV))
    gain = jnp.sqrt((data_energy + 1e-06) / (pred_energy + 1e-06))
    primaries = wavefield - gain[None, :, None, None] * multiples
    return (multiples, primaries)


def solution(mesh):
    split = Mesh(mesh.devices.reshape(4, 2, 2, 8, 2), ("src_0", "src_1", "rcv_0", "rcv_1", "rcv_2"))
    return jax.shard_map(
        per_device,
        mesh=split,
        in_specs=(P(None, None, RCV, SRC), P(None, RCV, None), P(RCV), P(RCV), P()),
        out_specs=(P(None, None, RCV, SRC), P(None, None, RCV, SRC)),
        check_vma=False,
    )
```

profile of v0, /device:TPU:1, one launch (start us, length us, event | category | flops | bytes accessed | tf_op | source)
XLA Modules:
  0.0 115.4 jit_solution(8125680364762427383)
XLA Ops:
  1.3 2.0 %multiply_reduce_fusion.1 = (f32[16]{0:T(128)S(1)}, f32[2,16,64,256]{3,2,1,0:T(8,128)S(1)}) fusion(f32[2,16,64,256]{3,2,1,0:T(8,128)} %param.5, f32[64]{0:T(128)S(1)} %convert_element_type.4), kind=kLoop, calls=%fused_computation.25 | loop fusion | flops 1572848 | bytes 4194624 | tf_op jit(solution)/shard_map/reduce_sum | solution.py:86
  3.3 2.1 %fusion.32 = (f32[2,16,48,256]{3,2,1,0:T(8,128)}, f32[2,16,48,256]{3,2,1,0:T(8,128)}) fusion(f32[2,16,64,256]{3,2,1,0:T(8,128)S(1)} %get-tuple-element.15), kind=kLoop, calls=%fused_computation.53 | loop fusion | bytes 6291456 | tf_op jit(solution)/shard_map/slice | solution.py:22
  5.3 5.1 %collective-permute-start.1 = (f32[2,16,48,256]{3,2,1,0:T(8,128)}, f32[2,16,48,256]{3,2,1,0:T(8,128)}, u32[]{:S(2)}, u32[]{:S(2)}) collective-permute-start(f32[2,16,48,256]{3,2,1,0:T(8,128)} %get-tuple-element.20), channel_id=1, source_target_pairs={{1,0},{2,1},{3,2},{4,3},{5,4},{6,5},{7,6},{8,7},{9,8},{10,9},{11,1... | collective-permute-start | bytes 4718600 | tf_op jit(solution)/shard_map/ppermute | solution.py:28
  10.4 1.9 %collective-permute-start = (f32[2,16,48,256]{3,2,1,0:T(8,128)}, f32[2,16,48,256]{3,2,1,0:T(8,128)}, u32[]{:S(2)}, u32[]{:S(2)}) collective-permute-start(f32[2,16,48,256]{3,2,1,0:T(8,128)} %get-tuple-element.21), channel_id=1, source_target_pairs={{0,1},{1,2},{2,3},{3,4},{4,5},{5,6},{6,7},{7,8},{8,9},{9,10},{10,1... | collective-permute-start | bytes 4718600 | tf_op jit(solution)/shard_map/ppermute | solution.py:26
  13.0 1.3 %reshape.28 = f32[2,64,16,64]{3,2,1,0:T(8,128)S(1)} reshape(f32[2,64,1024]{2,1,0:T(8,128)} %param.6) | data formatting | bytes 1048576 | tf_op jit(solution)/shard_map/reshape | solution.py:79
  15.7 13.0 %collective-permute-done.1 = f32[2,16,48,256]{3,2,1,0:T(8,128)} collective-permute-done((f32[2,16,48,256]{3,2,1,0:T(8,128)}, f32[2,16,48,256]{3,2,1,0:T(8,128)}, u32[]{:S(2)}, u32[]{:S(2)}) %collective-permute-start.1) | collective-permute-done | bytes 1572896 | tf_op jit(solution)/shard_map/ppermute | solution.py:28
  28.7 1.4 %collective-permute-done = f32[2,16,48,256]{3,2,1,0:T(8,128)} collective-permute-done((f32[2,16,48,256]{3,2,1,0:T(8,128)}, f32[2,16,48,256]{3,2,1,0:T(8,128)}, u32[]{:S(2)}, u32[]{:S(2)}) %collective-permute-start) | collective-permute-done | bytes 1572896 | tf_op jit(solution)/shard_map/ppermute | solution.py:26
  30.0 3.0 %fusion.1 = f32[2,16,127,256]{3,2,1,0:T(8,128)S(1)} fusion(s32[]{:T(128)S(6)} %select_n.3, f32[2,16,48,256]{3,2,1,0:T(8,128)} %collective-permute-done, f32[2,16,64,256]{3,2,1,0:T(8,128)S(1)} %get-tuple-element.15, f32[2,16,48,256]{3,2,1,0:T(8,128)} %collective-permute-done.1), kind=kLoop, calls=%fused_computation.4 | loop fusion | flops 2080768 | bytes 9404420 | tf_op jit(solution)/shard_map/concatenate | solution.py:24
  33.0 1.4 %fusion.12 = f32[16,64,256]{2,1,0:T(8,128)S(1)} fusion(f32[2,16,127,256]{3,2,1,0:T(8,128)S(1)} %fusion.1, f32[16,127,64]{1,0,2:T(8,128)S(1)} %get-tuple-element.22), kind=kOutput, calls=%fused_computation.31 | convolution fusion | flops 399507456 | bytes 3670016 | tf_op jit(solution)/shard_map/fjc,fjs->fcs/dot_general | solution.py:57
  34.4 1.4 %fusion.13 = f32[16,64,256]{2,1,0:T(8,128)S(1)} fusion(f32[2,16,127,256]{3,2,1,0:T(8,128)S(1)} %fusion.1, f32[16,127,64]{1,0,2:T(8,128)S(1)} %get-tuple-element.23), kind=kOutput, calls=%fused_computation.32 | convolution fusion | flops 399507456 | bytes 3670016 | tf_op jit(solution)/shard_map/fjc,fjs->fcs/dot_general | solution.py:54
  35.8 1.4 %fusion.20 = f32[1,16,64,256]{3,2,1,0:T(8,128)S(1)} fusion(f32[16,64,256]{2,1,0:T(8,128)S(1)} %fusion.12, f32[2,16,127,256]{3,2,1,0:T(8,128)S(1)} %fusion.1, f32[16,127,64]{1,0,2:T(8,128)S(1)} %get-tuple-element.23), kind=kOutput, calls=%fused_computation.37 | convolution fusion | flops 399769600 | bytes 4718592 | tf_op jit(solution)/shard_map/fjc,fjs->fcs/dot_general | solution.py:55
  37.3 1.4 %fusion.18 = f32[1,16,64,256]{3,2,1,0:T(8,128)S(1)} fusion(f32[16,64,256]{2,1,0:T(8,128)S(1)} %fusion.13, f32[2,16,127,256]{3,2,1,0:T(8,128)S(1)} %fusion.1, f32[16,127,64]{1,0,2:T(8,128)S(1)} %get-tuple-element.22), kind=kOutput, calls=%fused_computation.35 | convolution fusion | flops 399769600 | bytes 4718592 | tf_op jit(solution)/shard_map/fjc,fjs->fcs/dot_general | solution.py:52
  38.7 1.4 %fusion.21 = (f32[2,16,64,2]{3,2,1,0:T(8,128)}, f32[2,16,64,2]{3,2,1,0:T(8,128)S(1)}) fusion(f32[1,16,64,256]{3,2,1,0:T(8,128)S(1)} %fusion.18, f32[1,16,64,256]{3,2,1,0:T(8,128)S(1)} %fusion.20), kind=kLoop, calls=%fused_computation.38 | loop fusion | flops 8192 | bytes 2129920 | tf_op jit(solution)/shard_map/stack | solution.py:58
  40.0 1.6 %copy.17 = f32[2,16,64,2]{2,1,3,0:T(8,128)S(1)} copy(f32[2,16,64,2]{3,2,1,0:T(8,128)} %get-tuple-element.18) | data formatting | bytes 32768 | tf_op jit(solution)/shard_map/slice | solution.py:23
  43.3 5.7 %collective-permute-start.2 = (f32[2,16,64,2]{2,1,3,0:T(8,128)S(1)}, f32[2,16,64,2]{2,1,3,0:T(8,128)S(1)}, u32[]{:S(2)}, u32[]{:S(2)}) collective-permute-start(f32[2,16,64,2]{2,1,3,0:T(8,128)S(1)} %copy.17), channel_id=1, source_target_pairs={{0,32},{32,64},{64,96},{96,128},{128,160},{160,192},{192,224},{1,3... | collective-permute-start | bytes 49160 | tf_op jit(solution)/shard_map/ppermute | solution.py:26
  50.2 1.4 %copy.20 = f32[2,16,64,2]{3,2,1,0:T(8,128)} copy(f32[2,16,64,2]{2,1,3,0:T(8,128)S(1)} %collective-permute-done.3) | data formatting | bytes 32768 | tf_op jit(solution)/shard_map/ppermute | solution.py:28
  51.6 2.3 %maximum_maximum_fusion = (f32[2,16,64,258]{3,2,1,0:T(8,128)S(1)}, f32[2,16,64,258]{3,2,1,0:T(8,128)S(1)}) fusion(f32[1,16,64,256]{3,2,1,0:T(8,128)S(1)} %fusion.20, f32[1,16,64,256]{3,2,1,0:T(8,128)S(1)} %fusion.18, f32[2,16,64,2]{3,2,1,0:T(8,128)S(1)} %copy.18, f32[2,16,64,2]{3,2,1,0:T(8,128)} %copy.20), kind=kLoop, calls=%fused_computation.5 | loop fusion | flops 2113536 | bytes 6356992 | tf_op jit(solution)/shard_map/concatenate | solution.py:24
  54.0 6.2 %multiply_reduce_fusion = (f32[16]{0:T(128)S(1)}, f32[2,16,64,256]{3,2,1,0:T(8,128)}) fusion(f32[2,16,64,258]{3,2,1,0:T(8,128)S(1)} %get-tuple-element.17, f32[]{:T(128)} %bitcast.16, f32[]{:T(128)} %bitcast.15, f32[1,16,64,256]{3,2,1,0:T(8,128)S(1)} %fusion.20, f32[1,16,64,256]{3,2,1,0:T(8,128)S(1)} %fusion.18, f32[]{:T(128)} %bitcast.14, ...), kind=kLoop, calls=%fused_computation.24 | loop fusion | flops 6291440 | bytes 12582996 | tf_op jit(solution)/shard_map/reduce_sum | solution.py:87
  60.2 12.6 %all-reduce.1 = (f32[16]{0:T(128)S(1)}, f32[16]{0:T(128)S(1)}) all-reduce(f32[16]{0:T(128)S(1)} %get-tuple-element.12, f32[16]{0:T(128)S(1)} %get-tuple-element.14), channel_id=1, replica_groups=mesh['src_0'=4,'src_1'=2,'rcv_0'=2,'rcv_1'=8,'rcv_2'=2] {'src_0'}, use_global_device_ids=true, to_apply=%region_7.0 | all-reduce | flops 32 | bytes 256 | tf_op jit(solution)/shard_map/psum | solution.py:36
  72.8 5.3 %all-reduce.4 = (f32[16]{0:T(128)S(1)}, f32[16]{0:T(128)S(1)}) all-reduce(f32[16]{0:T(128)S(1)} %get-tuple-element.4, f32[16]{0:T(128)S(1)} %get-tuple-element.5), channel_id=1, replica_groups=mesh['src_0'=4,'src_1'=2,'rcv_0'=2,'rcv_1'=8,'rcv_2'=2] {'src_1'}, use_global_device_ids=true, to_apply=%region_8.0 | all-reduce | flops 32 | bytes 256 | tf_op jit(solution)/shard_map/psum | solution.py:36
  78.1 3.8 %all-reduce.3 = (f32[16]{0:T(128)S(1)}, f32[16]{0:T(128)S(1)}) all-reduce(f32[16]{0:T(128)S(1)} %get-tuple-element.10, f32[16]{0:T(128)S(1)} %get-tuple-element.11), channel_id=1, replica_groups=mesh['src_0'=4,'src_1'=2,'rcv_0'=2,'rcv_1'=8,'rcv_2'=2] {'rcv_0'}, use_global_device_ids=true, to_apply=%region_9.0 | all-reduce | flops 32 | bytes 256 | tf_op jit(solution)/shard_map/psum | solution.py:36
  81.8 18.2 %all-reduce = (f32[16]{0:T(128)S(1)}, f32[16]{0:T(128)S(1)}) all-reduce(f32[16]{0:T(128)S(1)} %get-tuple-element.8, f32[16]{0:T(128)S(1)} %get-tuple-element.9), channel_id=1, replica_groups=mesh['src_0'=4,'src_1'=2,'rcv_0'=2,'rcv_1'=8,'rcv_2'=2] {'rcv_1'}, use_global_device_ids=true, to_apply=%region_10.0 | all-reduce | flops 32 | bytes 256 | tf_op jit(solution)/shard_map/psum | solution.py:36
  100.0 11.2 %all-reduce.2 = (f32[16]{0:T(128)S(1)}, f32[16]{0:T(128)S(1)}) all-reduce(f32[16]{0:T(128)S(1)} %get-tuple-element.2, f32[16]{0:T(128)S(1)} %get-tuple-element.3), channel_id=1, replica_groups=mesh['src_0'=4,'src_1'=2,'rcv_0'=2,'rcv_1'=8,'rcv_2'=2] {'rcv_2'}, use_global_device_ids=true, to_apply=%region_11.0 | all-reduce | flops 32 | bytes 256 | tf_op jit(solution)/shard_map/psum | solution.py:36
  111.3 4.1 %multiply_subtract_fusion = f32[2,16,64,256]{3,2,1,0:T(8,128)} fusion(f32[2,16,64,256]{3,2,1,0:T(8,128)} %param.5, f32[2,16,64,256]{3,2,1,0:T(8,128)} %get-tuple-element.13, f32[16]{0:T(128)S(1)} %fusion.30), kind=kLoop, calls=%fused_computation.23 | loop fusion | flops 1048576 | bytes 6291520 | tf_op jit(solution)/shard_map/sub | solution.py:90
  (13 shorter events, 4.9 us)
Async XLA Ops:
  5.3 23.3 %collective-permute-start.1 = (f32[2,16,48,256]{3,2,1,0:T(8,128)}, f32[2,16,48,256]{3,2,1,0:T(8,128)}, u32[]{:S(2)}, u32[]{:S(2)}) collective-permute-start(f32[2,16,48,256]{3,2,1,0:T(8,128)} %get-tuple-element.20), channel_id=1, source_target_pairs={{1,0},{2,1},{3,2},{4,3},{5,4},{6,5},{7,6},{8,7},{9,8},{10,9},{11,1... | collective-permute-start | bytes 4718600 | tf_op jit(solution)/shard_map/ppermute | solution.py:28
  10.4 19.6 %collective-permute-start = (f32[2,16,48,256]{3,2,1,0:T(8,128)}, f32[2,16,48,256]{3,2,1,0:T(8,128)}, u32[]{:S(2)}, u32[]{:S(2)}) collective-permute-start(f32[2,16,48,256]{3,2,1,0:T(8,128)} %get-tuple-element.21), channel_id=1, source_target_pairs={{0,1},{1,2},{2,3},{3,4},{4,5},{5,6},{6,7},{7,8},{8,9},{9,10},{10,1... | collective-permute-start | bytes 4718600 | tf_op jit(solution)/shard_map/ppermute | solution.py:26
  40.0 9.0 %copy-start = (f32[5]{0:T(128)S(1)}, f32[5]{0:T(128)}, u32[]{:S(2)}) copy-start(f32[5]{0:T(128)} %param.9) | copy-start | bytes 64
  42.0 8.2 %collective-permute-start.3 = (f32[2,16,64,2]{2,1,3,0:T(8,128)S(1)}, f32[2,16,64,2]{2,1,3,0:T(8,128)S(1)}, u32[]{:S(2)}, u32[]{:S(2)}) collective-permute-start(f32[2,16,64,2]{2,1,3,0:T(8,128)S(1)} %copy.19), channel_id=1, source_target_pairs={{32,0},{64,32},{96,64},{128,96},{160,128},{192,160},{224,192},{33,... | collective-permute-start | bytes 49160 | tf_op jit(solution)/shard_map/ppermute | solution.py:28
  43.3 6.5 %collective-permute-start.2 = (f32[2,16,64,2]{2,1,3,0:T(8,128)S(1)}, f32[2,16,64,2]{2,1,3,0:T(8,128)S(1)}, u32[]{:S(2)}, u32[]{:S(2)}) collective-permute-start(f32[2,16,64,2]{2,1,3,0:T(8,128)S(1)} %copy.17), channel_id=1, source_target_pairs={{0,32},{32,64},{64,96},{96,128},{128,160},{160,192},{192,224},{1,3... | collective-permute-start | bytes 49160 | tf_op jit(solution)/shard_map/ppermute | solution.py:26
where the time goes:
time: 116 us; the launch traced here: 115 us
  blocking collectives  51.1 us (44%)
  other arithmetic  19.7 us (17%)
  waiting for transfers between devices  14.5 us (12%)
  starting transfers between devices  14 us (12%)
  local copies, waits for them, and re-layouts  7.87 us (7%)
  matrix products  6.8 us (6%)
  between operations  1.43 us (1%)
    psum x5, blocking collectives, by_axis(): return functools.reduce(lax.psum, axes, array)  51.1 us
    ppermute x2, waiting for transfers between devices, extended(): lax.ppermute(head, axis, [((i + 1) % count, i) for i in range(ends)])  13 us
    ppermute x2, starting transfers between devices, extended(): lax.ppermute(tail, axis, [(i, (i + 1) % count) for i in range(ends)])  7.59 us
    ppermute x2, starting transfers between devices, extended(): lax.ppermute(head, axis, [((i + 1) % count, i) for i in range(ends)])  6.4 us
    reduce_sum x1, other arithmetic, per_device(): pred_energy = jnp.sum(multiples * multiples, axis=(0, 2, 3))  6.24 us
    concatenate x2, other arithmetic, extended(): jnp.concatenate([lax.ppermute(tail, axis, [(i, (i + 1) % count) for i in...  5.34 us
    sub x1, other arithmetic, per_device(): primaries = wavefield - gain[None, :, None, None] * multiples  4.1 us
    slice x2, local copies, waits for them, and re-layouts, extended(): head = lax.slice_in_dim(cells, 0, width, axis=dim)  2.45 us
  transfers between devices with their start and end apart: 4, of which 3 were waited for; matrix products, arithmetic and copies ran while one was open for 3% of the time, Pallas kernels for 0%

commit v1 on v0

v1 whole, which is shorter than its diff:
```python
import functools

import jax
import jax.numpy as jnp
from jax import lax
from jax.experimental import pallas as pl
from jax.experimental.pallas import tpu as pltpu
from jax.sharding import Mesh
from jax.sharding import PartitionSpec as P

APER = 64
LANES = 128
HALO = 48
RCV = ("rcv_0", "rcv_1", "rcv_2")
SRC = ("src_0", "src_1")
NEAR = ("rcv_1", "rcv_2")
FAR = ("src_0", "src_1", "rcv_0")
EARLY = 6
MESH = pl.DeviceIdType.MESH


def place(axes):
    index = 0
    for axis in axes:
        index = index * lax.axis_size(axis) + lax.axis_index(axis)
    return index


def count_of(axes):
    count = 1
    for axis in axes:
        count *= lax.axis_size(axis)
    return count


def at(axes, index):
    coordinates = {}
    for axis in reversed(axes):
        coordinates[axis] = lax.rem(index, lax.axis_size(axis))
        index = index // lax.axis_size(axis)
    return coordinates


def beside(axes, step):
    count = count_of(axes)
    return at(axes, lax.rem(place(axes) + (step + count), count))


def lanes_of(shape):
    return lax.broadcasted_iota(jnp.int32, shape, 1)


def taper(h, x0, x1, weights):
    lane = lanes_of(x0.shape)
    first, last = lane == 0, lane == LANES - 1

    def later(a, b0, b1):
        ra, r0, r1 = (pltpu.roll(v, 1, 1) for v in (a, b0, b1))
        return ra, jnp.where(first, ra, r0), jnp.where(first, r0, r1)

    def sooner(a, b0, b1):
        ra, r0, r1 = (pltpu.roll(v, LANES - 1, 1) for v in (a, b0, b1))
        return ra, jnp.where(last, r1, r0), jnp.where(last, ra, r1)

    parts = (h, x0, x1)
    below = later(*(weights[0] * v for v in parts))
    below = later(*(s + weights[1] * v for s, v in zip(below, parts)))
    above = sooner(*(weights[4] * v for v in parts))
    above = sooner(*(s + weights[3] * v for s, v in zip(above, parts)))
    return tuple(below[i] + weights[2] * parts[i] + above[i] for i in (1, 2))


def halves(value):
    high = value.astype(jnp.bfloat16)
    return high, (value - high.astype(jnp.float32)).astype(jnp.bfloat16)


def kernel(
    x_hbm, band_hbm, shift_ref, mask_hbm, taper_ref,
    mult_ref, prim_ref,
    xv, bandv, mask_own, mask_left, mask_right, edges, edges_left, edges_right,
    rim, rim_left, rim_right, left, right, bands, high, low, row, near, far,
    x_sem, band_sem, mask_sem, send_sem, left_sem, right_sem, aux_send, aux_recv,
    near_send, near_recv, far_send, far_recv,
):
    slices = xv.shape[1]
    groups = x_sem.shape[0]
    per_group = slices // groups
    weights = [taper_ref[i] for i in range(5)]
    shift = shift_ref[0]

    def fetch(g):
        part = pl.ds(g * per_group, per_group)
        return pltpu.make_async_copy(x_hbm.at[:, part], xv.at[:, part], x_sem.at[g])

    for g in range(groups):
        fetch(g).start()
    mask_copy = pltpu.make_async_copy(mask_hbm, mask_own, mask_sem)
    mask_copy.start()
    band_copy = pltpu.make_async_copy(band_hbm, bandv, band_sem)
    band_copy.start()

    before, after = beside(RCV, -1), beside(RCV, 1)
    near_count, far_count = count_of(NEAR), count_of(FAR)
    near_me, far_me = place(NEAR), place(FAR)
    barrier = pltpu.get_barrier_semaphore()
    pl.semaphore_signal(barrier, inc=1, device_id=before, device_id_type=MESH)
    pl.semaphore_signal(barrier, inc=1, device_id=after, device_id_type=MESH)
    for axes, count in ((NEAR, near_count), (FAR, far_count)):
        @pl.loop(1, count)
        def _(step):
            pl.semaphore_signal(barrier, inc=1, device_id=beside(axes, step), device_id_type=MESH)

    for g in range(groups):
        fetch(g).wait()
    mask_copy.wait()

    def pack(p, packed):
        c, f = p // slices, lax.rem(p, slices)
        x0, x1 = xv[c, f, :, :LANES], xv[c, f, :, LANES:]
        lane = lanes_of(x0.shape)
        ends = jnp.where(lane < 2, x0, jnp.where(lane >= LANES - 2, x1, 0.0))
        return packed + pltpu.roll(ends, 4 * p + 2, 1)

    edges[...] = lax.fori_loop(0, 2 * slices, pack, jnp.zeros(edges.shape, jnp.float32))
    pl.semaphore_wait(barrier, 2 + (near_count - 1) + (far_count - 1))

    def to_left(f):
        return pltpu.make_async_remote_copy(
            src_ref=xv.at[:, f, pl.ds(0, HALO)], dst_ref=right.at[f],
            send_sem=send_sem.at[0, f], recv_sem=right_sem.at[f],
            device_id=before, device_id_type=MESH)

    def to_right(f):
        return pltpu.make_async_remote_copy(
            src_ref=xv.at[:, f, pl.ds(BLOCK_ROWS - HALO, HALO)], dst_ref=left.at[f],
            send_sem=send_sem.at[1, f], recv_sem=left_sem.at[f],
            device_id=after, device_id_type=MESH)

    def aux(i, source, target, device):
        return pltpu.make_async_remote_copy(
            src_ref=source, dst_ref=target, send_sem=aux_send.at[i], recv_sem=aux_recv.at[i],
            device_id=device, device_id_type=MESH)

    mask_copies = (aux(0, mask_own, mask_right, before), aux(1, mask_own, mask_left, after))
    edge_copies = (aux(2, edges, edges_right, beside(SRC, -1)), aux(3, edges, edges_left, beside(SRC, 1)))
    rim_copies = (
        aux(4, rim.at[pl.ds(0, HALO)], rim_right, before),
        aux(5, rim.at[pl.ds(BLOCK_ROWS - HALO, HALO)], rim_left, after))
    for copy in mask_copies:
        copy.start()

    @pl.loop(0, EARLY)
    def _(f):
        to_left(f).start()
        to_right(f).start()

    for copy in edge_copies:
        copy.start()

    lane_row = lanes_of((1, LANES))

    def data_part(f, energy):
        x = xv[:, f]
        return jnp.where(lane_row == f, jnp.sum(x * x), energy)

    energy = lax.fori_loop(0, slices, data_part, jnp.zeros((1, LANES), jnp.float32))

    for copy in mask_copies:
        copy.wait_recv()
    place_r, count_r = place(RCV), count_of(RCV)
    has_left = (place_r > 0).astype(jnp.float32)
    has_right = (place_r < count_r - 1).astype(jnp.float32)
    lane_half = lanes_of((1, BLOCK_ROWS))
    m_own = mask_own[...].astype(jnp.float32)
    m_left = mask_left[...].astype(jnp.float32) * has_left
    m_right = mask_right[...].astype(jnp.float32) * has_right
    mask = jnp.concatenate([m_own, jnp.where(lane_half <= 30 + shift, m_right, m_left)], axis=1)

    band_copy.wait()

    @pl.loop(0, slices // 2)
    def _(g):
        lane = lanes_of((BLOCK_ROWS, LANES))
        for odd in range(2):
            f = 2 * g + odd
            pieces = []
            for c in range(2):
                tile = bandv[c, :, pl.ds(pl.multiple_of(g * LANES, LANES), LANES)]
                tile = jnp.where((lane >= APER) if odd else (lane < APER), tile, 0.0)
                turn = shift + (LANES - APER // 2 - odd * APER)
                tile = pltpu.roll(pltpu.roll(tile, turn, 1), 0, 1, stride=1, stride_axis=0)
                pieces.append(halves(tile * mask))
            for k in range(2):
                real, imag = pieces[0][k], pieces[1][k]
                base = 2 * BLOCK_ROWS * k
                bands[f, base:base + BLOCK_ROWS, :LANES] = real
                bands[f, base:base + BLOCK_ROWS, LANES:] = -imag
                bands[f, base + BLOCK_ROWS:base + 2 * BLOCK_ROWS, :LANES] = imag
                bands[f, base + BLOCK_ROWS:base + 2 * BLOCK_ROWS, LANES:] = real

    for copy in edge_copies:
        copy.wait_recv()
    place_s, count_s = place(SRC), count_of(SRC)
    lane = lanes_of(edges.shape)
    from_left = edges_left[...] * (place_s > 0).astype(jnp.float32)
    from_right = edges_right[...] * (place_s < count_s - 1).astype(jnp.float32)
    rim[...] = jnp.where(lax.rem(lane, 4) < 2, from_left, from_right)
    for copy in rim_copies:
        copy.start()

    @pl.loop(EARLY, slices)
    def _(f):
        to_left(f).start()
        to_right(f).start()

    def put(f, c, rows, values):
        for side, value in enumerate(values):
            h, l = halves(value)
            high[f, pl.ds(c * LANES + rows, BLOCK_ROWS), side * LANES:(side + 1) * LANES] = h
            low[f, pl.ds(c * LANES + rows, BLOCK_ROWS), side * LANES:(side + 1) * LANES] = l

    @pl.loop(0, slices)
    def _(f):
        for c in range(2):
            h = pltpu.roll(rim[...], LANES - 2 - 4 * (c * slices + f), 1)
            put(f, c, 0, taper(h, xv[c, f, :, :LANES], xv[c, f, :, LANES:], weights))

    for copy in rim_copies:
        copy.wait_recv()

    def blend(r, l):
        rows = lax.broadcasted_iota(jnp.int32, (32, r.shape[1]), 0) + 16
        return jnp.concatenate([r[:16], jnp.where(rows <= 30 + shift, r[16:], l[:32]), l[32:]], axis=0)

    rim_halo = blend(rim_right[...], rim_left[...])

    def finish(f, energy):
        to_left(f).wait_recv()
        to_right(f).wait_recv()
        for c in range(2):
            h = pltpu.roll(rim_halo, LANES - 2 - 4 * (c * slices + f), 1)
            x = blend(right[f, c], left[f, c])
            put(f, c, BLOCK_ROWS, taper(h, x[:, :LANES], x[:, LANES:], weights))
        wide = jnp.dot(bands[f], high[f], preferred_element_type=jnp.float32)
        thin = jnp.dot(bands[f, :LANES], low[f], preferred_element_type=jnp.float32)
        result = wide[:LANES] + wide[LANES:] + thin
        mult_ref[0, f] = result[:BLOCK_ROWS]
        mult_ref[1, f] = result[BLOCK_ROWS:]
        return jnp.where(lane_row == f + slices, jnp.sum(result * result), energy)

    energy = lax.fori_loop(0, slices, finish, energy)

    def total(axes, me, count, slots, sends, recvs, energy, stage):
        row[stage] = energy
        slots[me] = energy

        def copy(step):
            return pltpu.make_async_remote_copy(
                src_ref=row.at[stage], dst_ref=slots.at[me], send_sem=sends.at[step], recv_sem=recvs.at[me],
                device_id=beside(axes, step), device_id_type=MESH)

        def arrival(step):
            other = lax.rem(me + step, count)
            return pltpu.make_async_remote_copy(
                src_ref=row.at[stage], dst_ref=slots.at[other], send_sem=sends.at[step], recv_sem=recvs.at[other],
                device_id=beside(axes, step), device_id_type=MESH)

        @pl.loop(1, count)
        def _(step):
            copy(step).start()

        @pl.loop(1, count)
        def _(step):
            arrival(step).wait_recv()

        result = slots[0]
        for slot in range(1, count):
            result = result + slots[slot]

        @pl.loop(1, count)
        def _(step):
            copy(step).wait_send()

        return result

    energy = total(NEAR, near_me, near_count, near, near_send, near_recv, energy, 0)
    energy = total(FAR, far_me, far_count, far, far_send, far_recv, energy, 1)
    predicted = pltpu.roll(energy, LANES - slices, 1)
    gain = jnp.sqrt((energy + 1e-06) / (predicted + 1e-06))

    @pl.loop(0, slices)
    def _(f):
        scale = jnp.sum(jnp.where(lane_row == f, gain, 0.0))
        prim_ref[:, f] = xv[:, f] - scale * mult_ref[:, f]

    for copy in mask_copies + edge_copies + rim_copies:
        copy.wait_send()

    @pl.loop(0, slices)
    def _(f):
        to_left(f).wait_send()
        to_right(f).wait_send()


BLOCK_ROWS = 64


def per_device(wavefield, surface_band, band_shift, trace_mask, shot_taper):
    _, slices, receivers, shots = wavefield.shape
    near_count, far_count = count_of(NEAR), count_of(FAR)
    groups = 4
    anywhere = pl.BlockSpec(memory_space=pl.ANY)
    scalars = pl.BlockSpec(memory_space=pltpu.SMEM)
    whole = pl.BlockSpec(memory_space=pltpu.VMEM)
    f32, bf16 = jnp.float32, jnp.bfloat16
    dma = pltpu.SemaphoreType.DMA
    return pl.pallas_call(
        kernel,
        out_shape=(jax.ShapeDtypeStruct(wavefield.shape, f32),) * 2,
        in_specs=[anywhere, anywhere, scalars, anywhere, scalars],
        out_specs=(whole, whole),
        scratch_shapes=[
            pltpu.VMEM(wavefield.shape, f32),
            pltpu.VMEM(surface_band.shape, f32),
            pltpu.VMEM((1, receivers), jnp.int32),
            pltpu.VMEM((1, receivers), jnp.int32),
            pltpu.VMEM((1, receivers), jnp.int32),
            pltpu.VMEM((receivers, LANES), f32),
            pltpu.VMEM((receivers, LANES), f32),
            pltpu.VMEM((receivers, LANES), f32),
            pltpu.VMEM((receivers, LANES), f32),
            pltpu.VMEM((HALO, LANES), f32),
            pltpu.VMEM((HALO, LANES), f32),
            pltpu.VMEM((slices, 2, HALO, shots), f32),
            pltpu.VMEM((slices, 2, HALO, shots), f32),
            pltpu.VMEM((slices, 4 * receivers, 2 * LANES), bf16),
            pltpu.VMEM((slices, 2 * LANES, shots), bf16),
            pltpu.VMEM((slices, 2 * LANES, shots), bf16),
            pltpu.VMEM((2, 1, LANES), f32),
            pltpu.VMEM((near_count, 1, LANES), f32),
            pltpu.VMEM((far_count, 1, LANES), f32),
            dma((groups,)),
            dma(()),
            dma(()),
            dma((2, slices)),
            dma((slices,)),
            dma((slices,)),
            dma((6,)),
            dma((6,)),
            dma((near_count,)),
            dma((near_count,)),
            dma((far_count,)),
            dma((far_count,)),
        ],
        compiler_params=pltpu.CompilerParams(
            collective_id=0, has_side_effects=True, vmem_limit_bytes=48 * 1024 * 1024),
        name="predict",
    )(wavefield, surface_band, band_shift, trace_mask.reshape(1, receivers), shot_taper)


def solution(mesh):
    sizes = SPLIT_SIZES or (4, 2, 2, 8, 2)
    split = Mesh(mesh.devices.reshape(sizes), SRC + RCV)
    return jax.shard_map(
        per_device,
        mesh=split,
        in_specs=(P(None, None, RCV, SRC), P(None, RCV, None), P(RCV), P(RCV), P()),
        out_specs=(P(None, None, RCV, SRC), P(None, None, RCV, SRC)),
        check_vma=False,
    )


SPLIT_SIZES = None
```

time: 116 us -> 67.7 us (0.58)
  Pallas kernels: 0 us -> 61.2 us
  blocking collectives: 51.1 us -> 0 us
  other arithmetic: 19.7 us -> 0 us
  waiting for transfers between devices: 14.5 us -> 0 us
  starting transfers between devices: 14 us -> 0 us
  matrix products: 6.8 us -> 0 us
  local copies, waits for them, and re-layouts: 7.87 us -> 4.98 us
    pallas_call x0 -> x1, Pallas kernels: none -> 61.2 us  [per_device(): pl.pallas_call(kernel, out_shape=(jax.ShapeDtypeStruct(wavefield.shape, f...]
    psum x5 -> x0, blocking collectives: 51.1 us -> none  [by_axis(): return functools.reduce(lax.psum, axes, array)]
    ppermute x4 -> x0, waiting for transfers between devices: 14.5 us -> none  [the longest x2 13 us: extended(): lax.ppermute(head, axis, [((i + 1) % count, i) for i in range(ends)])]
    ppermute x4 -> x0, starting transfers between devices: 14 us -> none  [the longest x2 7.59 us: extended(): lax.ppermute(tail, axis, [(i, (i + 1) % count) for i in range(ends)])]
    reduce_sum x2 -> x0, other arithmetic: 8.22 us -> none  [the longest x1 6.24 us: per_device(): pred_energy = jnp.sum(multiples * multiples, axis=(0, 2, 3))]
    dot_general x5 -> x0, matrix products: 6.8 us -> none  [the longest x1 1.4 us: complex_product(): jnp.einsum('fjc,fjs->fcs', band[1], window[0], precision=lax.Precision.HI...]
    concatenate x2 -> x0, other arithmetic: 5.34 us -> none  [extended(): jnp.concatenate([lax.ppermute(tail, axis, [(i, (i + 1) % count) for i in...]
    unnamed x2 -> x8, local copies, waits for them, and re-layouts: 0.01 us -> 4.98 us
  transfers between devices with their start and end apart: 4 -> 0, of which waited for: 3 -> 0; matrix products, arithmetic and copies ran while one was open for 3% -> 0% of each run, Pallas kernels for 0% -> 0%
where the time goes in v1:
time: 67.7 us; the launch traced here: 67.5 us
  Pallas kernels  61.2 us (90%)
  local copies, waits for them, and re-layouts  4.98 us (7%)
  between operations  1.3 us (2%)
    pallas_call x1, Pallas kernels, per_device(): pl.pallas_call(kernel, out_shape=(jax.ShapeDtypeStruct(wavefield.shape, f...  61.2 us
    unnamed x8, local copies, waits for them, and re-layouts  4.98 us

profile of v1, /device:TPU:1, one launch (start us, length us, event | category | flops | bytes accessed | tf_op | source)
XLA Modules:
  0.0 67.5 jit_solution(17867663222326109855)
XLA Ops:
  1.3 0.0 copy-start
  1.3 1.0 %copy-done = f32[2,64,1024]{2,1,0:T(8,128)S(1)} copy-done((f32[2,64,1024]{2,1,0:T(8,128)S(1)}, f32[2,64,1024]{2,1,0:T(8,128)}, u32[]{:S(2)}) %copy-start) | copy-done | bytes 524312
  2.3 0.0 copy-start.1
  2.3 0.7 copy-done.1
  3.0 0.0 copy-start.2
  3.0 0.7 copy-done.2
  3.6 61.2 %predict.1 = (f32[2,16,64,256]{3,2,1,0:T(8,128)S(1)}, f32[2,16,64,256]{3,2,1,0:T(8,128)S(1)}) custom-call(f32[2,16,64,256]{3,2,1,0:T(8,128)} %x_hbm.1, f32[2,64,1024]{2,1,0:T(8,128)S(1)} %copy-done, s32[1]{0:T(128)S(6)} %copy.9.shift_ref, s32[1,64]{1,0:T(1,128)S(1)} %bitcast.1, f32[5]{0:T(128)S(1)} %copy-done.2), custom_call_target="tpu_custom_call" | custom-call | tf_op jit(solution)/shard_map/predict/pallas_call | solution.py:318
  64.9 1.3 %copy.10 = f32[2,16,64,256]{3,2,1,0:T(8,128)} copy(f32[2,16,64,256]{3,2,1,0:T(8,128)S(1)} %get-tuple-element.4) | data formatting | bytes 4194304
  66.2 1.3 %copy.11 = f32[2,16,64,256]{3,2,1,0:T(8,128)} copy(f32[2,16,64,256]{3,2,1,0:T(8,128)S(1)} %get-tuple-element.5) | data formatting | bytes 4194304
Async XLA Ops:
  1.3 1.0 %copy-start = (f32[2,64,1024]{2,1,0:T(8,128)S(1)}, f32[2,64,1024]{2,1,0:T(8,128)}, u32[]{:S(2)}) copy-start(f32[2,64,1024]{2,1,0:T(8,128)} %band_hbm.1) | copy-start | bytes 1572868
  2.3 0.7 copy-start.1
  3.0 0.7 copy-start.2

commit v2 on v1

v2 whole, which is shorter than its diff:
```python
import jax
import jax.numpy as jnp
from jax import lax
from jax.experimental import pallas as pl
from jax.experimental.pallas import tpu as pltpu
from jax.sharding import Mesh
from jax.sharding import PartitionSpec as P

APER = 64
LANES = 128
ROWS = 64
HALO = 48
RCV = ("rcv_0", "rcv_1", "rcv_2")
SRC = ("src_0", "src_1")
NEAR = ("rcv_1", "rcv_2")
FAR = ("src_0", "src_1", "rcv_0")
EARLY = 6
EARLY_FAR = 3
GROUPS = 4
MESH = pl.DeviceIdType.MESH
SPLIT_SIZES = (4, 2, 2, 8, 2)


def place(axes):
    index = 0
    for axis in axes:
        index = index * lax.axis_size(axis) + lax.axis_index(axis)
    return index


def count_of(axes):
    count = 1
    for axis in axes:
        count *= lax.axis_size(axis)
    return count


def at(axes, index):
    coordinates = {}
    for axis in reversed(axes):
        coordinates[axis] = lax.rem(index, lax.axis_size(axis))
        index = index // lax.axis_size(axis)
    return coordinates


def beside(axes, step):
    count = count_of(axes)
    return at(axes, lax.rem(place(axes) + (step + count), count))


def lanes_of(shape):
    return lax.broadcasted_iota(jnp.int32, shape, 1)


def rows_of(shape):
    return lax.broadcasted_iota(jnp.int32, shape, 0)


def taper(h, x0, x1, weights):
    lane = lanes_of(x0.shape)
    y0, y1 = weights[2] * x0, weights[2] * x1
    for step in (1, 2):
        wrap = lane >= LANES - step
        y0 += weights[2 - step] * pltpu.roll(jnp.where(wrap, h, x0), step, 1)
        y1 += weights[2 - step] * pltpu.roll(jnp.where(wrap, x0, x1), step, 1)
        wrap = lane < step
        y0 += weights[2 + step] * pltpu.roll(jnp.where(wrap, x1, x0), LANES - step, 1)
        y1 += weights[2 + step] * pltpu.roll(jnp.where(wrap, h, x1), LANES - step, 1)
    return y0, y1


def halves(value):
    high = value.astype(jnp.bfloat16)
    return high, (value - high.astype(jnp.float32)).astype(jnp.bfloat16)


def predict(
    x_hbm, band_hbm, shift_ref, mask_hbm, taper_hbm,
    xv, mult_ref, gain_ref,
    taper_ref, bandv, mask_own, mask_left, mask_right, edges, edges_left, edges_right,
    rim, rim_left, rim_right, left, right, bands, high, low, parts, row, near, far,
    x_sem, band_sem, mask_sem, taper_sem, send_sem, left_sem, right_sem, aux_send, aux_recv,
    near_send, near_recv, far_send, far_recv,
):
    slices = xv.shape[1]
    per_group = slices // GROUPS

    def fetch(g):
        part = pl.ds(g * per_group, per_group)
        return pltpu.make_async_copy(x_hbm.at[:, part], xv.at[:, part], x_sem.at[g])

    for g in range(GROUPS):
        fetch(g).start()
    mask_copy = pltpu.make_async_copy(mask_hbm, mask_own, mask_sem)
    mask_copy.start()
    band_copy = pltpu.make_async_copy(band_hbm, bandv, band_sem)
    band_copy.start()
    taper_copy = pltpu.make_async_copy(taper_hbm, taper_ref, taper_sem)
    taper_copy.start()

    before, after = beside(RCV, -1), beside(RCV, 1)
    has_before, has_after = place(RCV) > 0, place(RCV) < count_of(RCV) - 1
    has_lower, has_upper = place(SRC) > 0, place(SRC) < count_of(SRC) - 1
    near_count, far_count = count_of(NEAR), count_of(FAR)
    near_me, far_me = place(NEAR), place(FAR)
    barrier = pltpu.get_barrier_semaphore()
    for flag, device in ((has_before, before), (has_after, after)):
        @pl.when(flag)
        def _():
            pl.semaphore_signal(barrier, inc=1, device_id=device, device_id_type=MESH)
    for axes, count in ((NEAR, near_count), (FAR, far_count)):
        @pl.loop(1, count)
        def _(step):
            pl.semaphore_signal(barrier, inc=1, device_id=beside(axes, step), device_id_type=MESH)

    def to_left(f):
        return pltpu.make_async_remote_copy(
            src_ref=xv.at[:, f, pl.ds(0, HALO)], dst_ref=right.at[f],
            send_sem=send_sem.at[0, f], recv_sem=right_sem.at[f],
            device_id=before, device_id_type=MESH)

    def to_right(f):
        return pltpu.make_async_remote_copy(
            src_ref=xv.at[:, f, pl.ds(ROWS - HALO, HALO)], dst_ref=left.at[f],
            send_sem=send_sem.at[1, f], recv_sem=left_sem.at[f],
            device_id=after, device_id_type=MESH)

    def aux(i, source, target, device):
        return pltpu.make_async_remote_copy(
            src_ref=source, dst_ref=target, send_sem=aux_send.at[i], recv_sem=aux_recv.at[i],
            device_id=device, device_id_type=MESH)

    masks = ((aux(0, mask_own, mask_right, before), has_before, has_after),
             (aux(1, mask_own, mask_left, after), has_after, has_before))
    ends = ((aux(2, edges, edges_right, beside(SRC, -1)), has_lower, has_upper),
            (aux(3, edges, edges_left, beside(SRC, 1)), has_upper, has_lower))
    rims = ((aux(4, rim.at[pl.ds(0, HALO)], rim_right, before), has_before, has_after),
            (aux(5, rim.at[pl.ds(ROWS - HALO, HALO)], rim_left, after), has_after, has_before))

    def start(entries):
        for copy, sends, _ in entries:
            pl.when(sends)(copy.start)

    def arrive(entries):
        for copy, _, receives in entries:
            pl.when(receives)(copy.wait_recv)

    early_left = jnp.where(near_me == 0, EARLY_FAR, EARLY)
    early_right = jnp.where(near_me == near_count - 1, EARLY_FAR, EARLY)

    def bulk(copy, flag, first, last):
        @pl.when(flag)
        def _():
            @pl.loop(first, last)
            def _(f):
                copy(f).start()

    for g in range(GROUPS):
        fetch(g).wait()
    for copy in (mask_copy, taper_copy):
        copy.wait()
    weights = [taper_ref[i] for i in range(5)]
    shift = shift_ref[0]

    with jax.named_scope("pack"):
        def pack(f, packed):
            for c in range(2):
                x0, x1 = xv[c, f, :, :LANES], xv[c, f, :, LANES:]
                lane = lanes_of(x0.shape)
                tips = jnp.where(lane < 2, x0, jnp.where(lane >= LANES - 2, x1, 0.0))
                packed = packed + pltpu.roll(tips, 4 * (c * slices + f) + 2, 1)
            return packed

        edges[...] = lax.fori_loop(0, slices, pack, jnp.zeros(edges.shape, jnp.float32), unroll=4)

    with jax.named_scope("barrier"):
        neighbours = has_before.astype(jnp.int32) + has_after.astype(jnp.int32)
        pl.semaphore_wait(barrier, neighbours + (near_count - 1) + (far_count - 1))

    start(ends)
    start(masks)
    bulk(to_left, has_before, 0, early_left)
    bulk(to_right, has_after, 0, early_right)

    with jax.named_scope("clear"):
        @pl.when(jnp.logical_not(has_before))
        def _():
            mask_left[...] = jnp.zeros_like(mask_left)
            rim_left[...] = jnp.zeros_like(rim_left)
            left[...] = jnp.zeros_like(left)

        @pl.when(jnp.logical_not(has_after))
        def _():
            mask_right[...] = jnp.zeros_like(mask_right)
            rim_right[...] = jnp.zeros_like(rim_right)
            right[...] = jnp.zeros_like(right)

        @pl.when(jnp.logical_not(has_lower))
        def _():
            edges_left[...] = jnp.zeros_like(edges_left)

        @pl.when(jnp.logical_not(has_upper))
        def _():
            edges_right[...] = jnp.zeros_like(edges_right)

    with jax.named_scope("maskwait"):
        arrive(masks)
    lane_half = lanes_of((1, ROWS))
    m_own, m_left, m_right = (m[...].astype(jnp.float32) for m in (mask_own, mask_left, mask_right))
    mask = jnp.concatenate([m_own, jnp.where(lane_half <= 30 + shift, m_right, m_left)], axis=1)

    band_copy.wait()

    with jax.named_scope("bands"):
        @pl.loop(0, slices // 2)
        def _(g):
            lane = lanes_of((ROWS, LANES))
            for odd in range(2):
                f = 2 * g + odd
                pieces = []
                for c in range(2):
                    tile = bandv[c, :, pl.ds(pl.multiple_of(g * LANES, LANES), LANES)]
                    tile = jnp.where((lane >= APER) if odd else (lane < APER), tile, 0.0)
                    turn = shift + (LANES - APER // 2 - odd * APER)
                    tile = pltpu.roll(pltpu.roll(tile, turn, 1), 0, 1, stride=1, stride_axis=0)
                    pieces.append(halves(tile * mask))
                for k in range(2):
                    real, imag = pieces[0][k], pieces[1][k]
                    base = 2 * ROWS * k
                    bands[f, base:base + ROWS, :LANES] = real
                    bands[f, base:base + ROWS, LANES:] = -imag
                    bands[f, base + ROWS:base + 2 * ROWS, :LANES] = imag
                    bands[f, base + ROWS:base + 2 * ROWS, LANES:] = real

    with jax.named_scope("edgewait"):
        arrive(ends)
    rim[...] = jnp.where(lax.rem(lanes_of(rim.shape), 4) < 2, edges_left[...], edges_right[...])
    start(rims)
    bulk(to_left, has_before, early_left, slices)
    bulk(to_right, has_after, early_right, slices)

    def put(f, c, first, values):
        for side, value in enumerate(values):
            h, l = halves(value)
            columns = slice(side * LANES, (side + 1) * LANES)
            high[f, pl.ds(c * LANES + first, ROWS), columns] = h
            low[f, pl.ds(c * LANES + first, ROWS), columns] = l

    with jax.named_scope("own"):
        @pl.loop(0, slices)
        def _(f):
            squares = jnp.zeros((1, LANES), jnp.float32)
            for c in range(2):
                h = pltpu.roll(rim[...], LANES - 2 - 4 * (c * slices + f), 1)
                x0, x1 = xv[c, f, :, :LANES], xv[c, f, :, LANES:]
                put(f, c, 0, taper(h, x0, x1, weights))
                squares += jnp.sum(x0 * x0 + x1 * x1, axis=0, keepdims=True)
            parts[pl.ds(f, 1), :] = squares

    with jax.named_scope("rimwait"):
        arrive(rims)

    def blend(r, l):
        rows = rows_of((32, r.shape[1])) + 16
        return jnp.concatenate([r[:16], jnp.where(rows <= 30 + shift, r[16:], l[:32]), l[32:]], axis=0)

    rim_halo = blend(rim_right[...], rim_left[...])

    @pl.loop(0, slices)
    def _(f):
        with jax.named_scope("bulkwait"):
            pl.when(has_after)(to_left(f).wait_recv)
            pl.when(has_before)(to_right(f).wait_recv)
        for c in range(2):
            h = pltpu.roll(rim_halo, LANES - 2 - 4 * (c * slices + f), 1)
            x = blend(right[f, c], left[f, c])
            put(f, c, ROWS, taper(h, x[:, :LANES], x[:, LANES:], weights))
        wide = jnp.dot(bands[f], high[f], preferred_element_type=jnp.float32)
        thin = jnp.dot(bands[f, :LANES], low[f], preferred_element_type=jnp.float32)
        result = wide[:LANES] + wide[LANES:] + thin
        mult_ref[0, f] = result[:ROWS]
        mult_ref[1, f] = result[ROWS:]
        squares = jnp.sum(result * result, axis=0, keepdims=True)
        parts[pl.ds(slices + f, 1), :] = squares[:, :LANES] + squares[:, LANES:]

    shape = parts.shape
    diagonal = lanes_of(shape) == rows_of(shape)

    def to_row(column):
        return jnp.sum(jnp.where(diagonal, column, 0.0), axis=0, keepdims=True)

    def total(axes, me, count, slots, sends, recvs, energy, stage):
        row[stage] = energy
        slots[me] = energy

        def copy(step, slot):
            return pltpu.make_async_remote_copy(
                src_ref=row.at[stage], dst_ref=slots.at[slot], send_sem=sends.at[step], recv_sem=recvs.at[slot],
                device_id=beside(axes, step), device_id_type=MESH)

        @pl.loop(1, count)
        def _(step):
            copy(step, me).start()

        @pl.loop(1, count)
        def _(step):
            copy(step, lax.rem(me + step, count)).wait_recv()

        result = slots[0]
        for slot in range(1, count):
            result = result + slots[slot]
        return result

    energy = to_row(jnp.sum(parts[...], axis=1, keepdims=True))
    with jax.named_scope("near"):
        energy = total(NEAR, near_me, near_count, near, near_send, near_recv, energy, 0)
    with jax.named_scope("far"):
        energy = total(FAR, far_me, far_count, far, far_send, far_recv, energy, 1)
    predicted = pltpu.roll(energy, LANES - slices, 1)
    gain = jnp.sqrt((energy + 1e-06) / (predicted + 1e-06))
    spread = jnp.sum(jnp.where(diagonal[:slices], gain, 0.0), axis=1, keepdims=True)
    gain_ref[...] = jnp.broadcast_to(spread, gain_ref.shape)

    with jax.named_scope("sendwait"):
        for copy, sends, _ in masks + ends + rims:
            pl.when(sends)(copy.wait_send)

        @pl.when(has_before)
        def _():
            @pl.loop(0, slices)
            def _(f):
                to_left(f).wait_send()

        @pl.when(has_after)
        def _():
            @pl.loop(0, slices)
            def _(f):
                to_right(f).wait_send()

        for stage, (axes, count, sends) in enumerate(((NEAR, near_count, near_send), (FAR, far_count, far_send))):
            @pl.loop(1, count)
            def _(step):
                pltpu.make_async_remote_copy(
                    src_ref=row.at[stage], dst_ref=row.at[stage], send_sem=sends.at[step], recv_sem=sends.at[step],
                    device_id=beside(axes, step), device_id_type=MESH).wait_send()


def subtract(x_ref, mult_ref, gain_ref, mult_hbm, prim_hbm, prim, mult_sem, prim_sem):
    slices = prim.shape[1]
    per_group = slices // GROUPS

    def copy(source, target, sem, g):
        part = pl.ds(g * per_group, per_group)
        return pltpu.make_async_copy(source.at[:, part], target.at[:, part], sem.at[g])

    for g in range(GROUPS):
        copy(mult_ref, mult_hbm, mult_sem, g).start()
    for g in range(GROUPS):
        @pl.loop(g * per_group, (g + 1) * per_group)
        def _(f):
            scale = gain_ref[pl.ds(f, 1), :]
            for side in range(2):
                columns = slice(side * LANES, (side + 1) * LANES)
                for c in range(2):
                    prim[c, f, :, columns] = x_ref[c, f, :, columns] - scale * mult_ref[c, f, :, columns]

        copy(prim, prim_hbm, prim_sem, g).start()
    for g in range(GROUPS):
        copy(mult_ref, mult_hbm, mult_sem, g).wait()
        copy(prim, prim_hbm, prim_sem, g).wait()


def per_device(wavefield, surface_band, band_shift, trace_mask, shot_taper):
    _, slices, receivers, shots = wavefield.shape
    near_count, far_count = count_of(NEAR), count_of(FAR)
    hbm = pl.BlockSpec(memory_space=pltpu.HBM)
    scalars = pl.BlockSpec(memory_space=pltpu.SMEM)
    whole = pl.BlockSpec(memory_space=pltpu.VMEM)
    f32, bf16 = jnp.float32, jnp.bfloat16
    dma = pltpu.SemaphoreType.DMA
    field = jax.ShapeDtypeStruct(wavefield.shape, f32)
    wavefield, surface_band, trace_mask, shot_taper = (
        pltpu.with_memory_space_constraint(a, pltpu.HBM)
        for a in (wavefield, surface_band, trace_mask.reshape(1, receivers), shot_taper))
    held, multiples, gain = pl.pallas_call(
        predict,
        out_shape=(field, field, jax.ShapeDtypeStruct((slices, LANES), f32)),
        in_specs=[hbm, hbm, scalars, hbm, hbm],
        out_specs=(whole, whole, whole),
        scratch_shapes=[
            pltpu.SMEM(shot_taper.shape, f32),
            pltpu.VMEM(surface_band.shape, f32),
            pltpu.VMEM((1, receivers), jnp.int32),
            pltpu.VMEM((1, receivers), jnp.int32),
            pltpu.VMEM((1, receivers), jnp.int32),
            pltpu.VMEM((receivers, LANES), f32),
            pltpu.VMEM((receivers, LANES), f32),
            pltpu.VMEM((receivers, LANES), f32),
            pltpu.VMEM((receivers, LANES), f32),
            pltpu.VMEM((HALO, LANES), f32),
            pltpu.VMEM((HALO, LANES), f32),
            pltpu.VMEM((slices, 2, HALO, shots), f32),
            pltpu.VMEM((slices, 2, HALO, shots), f32),
            pltpu.VMEM((slices, 4 * receivers, 2 * LANES), bf16),
            pltpu.VMEM((slices, 2 * LANES, shots), bf16),
            pltpu.VMEM((slices, 2 * LANES, shots), bf16),
            pltpu.VMEM((2 * slices, LANES), f32),
            pltpu.VMEM((2, 1, LANES), f32),
            pltpu.VMEM((near_count, 1, LANES), f32),
            pltpu.VMEM((far_count, 1, LANES), f32),
            dma((GROUPS,)),
            dma(()),
            dma(()),
            dma(()),
            dma((2, slices)),
            dma((slices,)),
            dma((slices,)),
            dma((6,)),
            dma((6,)),
            dma((near_count,)),
            dma((near_count,)),
            dma((far_count,)),
            dma((far_count,)),
        ],
        compiler_params=pltpu.CompilerParams(
            collective_id=0, has_side_effects=True, vmem_limit_bytes=40 * 1024 * 1024),
        name="predict",
    )(wavefield, surface_band, band_shift, trace_mask, shot_taper)
    return pl.pallas_call(
        subtract,
        out_shape=(field, field),
        in_specs=[whole, whole, whole],
        out_specs=(hbm, hbm),
        scratch_shapes=[pltpu.VMEM(wavefield.shape, f32), dma((GROUPS,)), dma((GROUPS,))],
        compiler_params=pltpu.CompilerParams(vmem_limit_bytes=16 * 1024 * 1024),
        name="subtract",
    )(held, multiples, gain)


def solution(mesh):
    split = Mesh(mesh.devices.reshape(SPLIT_SIZES), SRC + RCV)
    return jax.shard_map(
        per_device,
        mesh=split,
        in_specs=(P(None, None, RCV, SRC), P(None, RCV, None), P(RCV), P(RCV), P()),
        out_specs=(P(None, None, RCV, SRC), P(None, None, RCV, SRC)),
        check_vma=False,
    )
```

time: 67.7 us -> 45.3 us (0.67)
  Pallas kernels: 61.2 us -> 43.9 us
  local copies, waits for them, and re-layouts: 4.98 us -> 0 us
    pallas_call x1 -> x2, Pallas kernels: 61.2 us -> 43.9 us  [the longest x1 41.8 us: per_device(): pl.pallas_call(predict, out_shape=(field, field, jax.ShapeDtypeStruct((sl...]
    unnamed x8 -> x0, local copies, waits for them, and re-layouts: 4.98 us -> none
where the time goes in v2:
time: 45.3 us; the launch traced here: 45.2 us
  Pallas kernels  43.9 us (97%)
  between operations  1.28 us (3%)
    pallas_call x1, Pallas kernels, per_device(): pl.pallas_call(predict, out_shape=(field, field, jax.ShapeDtypeStruct((sl...  41.8 us
    pallas_call x1, Pallas kernels, per_device(): pl.pallas_call(subtract, out_shape=(field, field), in_specs=[whole, whole...  2.07 us

profile of v2, /device:TPU:1, one launch (start us, length us, event | category | flops | bytes accessed | tf_op | source)
XLA Modules:
  0.0 45.2 jit_solution(3440168996309964304)
XLA Ops:
  1.3 41.8 %predict.1 = (f32[2,16,64,256]{3,2,1,0:T(8,128)S(1)}, f32[2,16,64,256]{3,2,1,0:T(8,128)S(1)}, f32[16,128]{1,0:T(8,128)S(1)}) custom-call(f32[2,16,64,256]{3,2,1,0:T(8,128)} %x_hbm.1, f32[2,64,1024]{2,1,0:T(8,128)} %band_hbm.1, s32[1]{0:T(128)S(6)} %copy.7.shift_ref, s32[1,64]{1,0:T(1,128)} %bitcast.1, f32[5]{0:T(128)} %taper_hbm.1), custom_call_target="tpu_custom_call" | custom-call | tf_op jit(solution)/shard_map/predict/pallas_call | solution.py:385
  43.1 2.1 %subtract.1 = (f32[2,16,64,256]{3,2,1,0:T(8,128)}, f32[2,16,64,256]{3,2,1,0:T(8,128)}) custom-call(f32[2,16,64,256]{3,2,1,0:T(8,128)S(1)} %get-tuple-element.5.x_ref, f32[2,16,64,256]{3,2,1,0:T(8,128)S(1)} %get-tuple-element.6.mult_ref, f32[16,128]{1,0:T(8,128)S(1)} %get-tuple-element.7.gain_ref), custom_call_target="tpu_custom_call" | custom-call | tf_op jit(solution)/shard_map/subtract/pallas_call | solution.py:429

commit v3 on v2

--- a/solution.py
+++ b/solution.py
@@ -14,7 +14,8 @@
 SRC = ("src_0", "src_1")
 NEAR = ("rcv_1", "rcv_2")
 FAR = ("src_0", "src_1", "rcv_0")
-EARLY = 6
+RINGS = (("src_0",), ("src_1", "rcv_0"), ("rcv_1",), ("rcv_2",))
+EARLY = 7
 EARLY_FAR = 3
 GROUPS = 4
 MESH = pl.DeviceIdType.MESH
@@ -46,6 +47,13 @@
 def beside(axes, step):
     count = count_of(axes)
     return at(axes, lax.rem(place(axes) + (step + count), count))
+
+
+def others_of(rings):
+    first, second = (count_of(ring) for ring in rings)
+    steps = [(i, j) for i in range(first) for j in range(second) if i or j]
+    steps.sort(key=lambda step: -min(step[0], first - step[0]) - min(step[1], second - step[1]))
+    return [{**beside(rings[0], i), **beside(rings[1], j)} for i, j in steps]
 
 
 def lanes_of(shape):
@@ -80,17 +88,17 @@
     taper_ref, bandv, mask_own, mask_left, mask_right, edges, edges_left, edges_right,
     rim, rim_left, rim_right, left, right, bands, high, low, parts, row, near, far,
     x_sem, band_sem, mask_sem, taper_sem, send_sem, left_sem, right_sem, aux_send, aux_recv,
-    near_send, near_recv, far_send, far_recv,
+    near_sem, far_sem, known,
 ):
     slices = xv.shape[1]
-    per_group = slices // GROUPS
-
-    def fetch(g):
-        part = pl.ds(g * per_group, per_group)
-        return pltpu.make_async_copy(x_hbm.at[:, part], xv.at[:, part], x_sem.at[g])
-
-    for g in range(GROUPS):
-        fetch(g).start()
+
+    def fetch(i, first, last):
+        part = pl.ds(first, last - first)
+        return pltpu.make_async_copy(x_hbm.at[:, part], xv.at[:, part], x_sem.at[i])
+
+    fetches = fetch(0, 0, slices // 2), fetch(1, slices // 2, slices)
+    for copy in fetches:
+        copy.start()
     mask_copy = pltpu.make_async_copy(mask_hbm, mask_own, mask_sem)
     mask_copy.start()
     band_copy = pltpu.make_async_copy(band_hbm, bandv, band_sem)
@@ -99,30 +107,46 @@
     taper_copy.start()
 
     before, after = beside(RCV, -1), beside(RCV, 1)
+    lower, upper = beside(SRC, -1), beside(SRC, 1)
     has_before, has_after = place(RCV) > 0, place(RCV) < count_of(RCV) - 1
     has_lower, has_upper = place(SRC) > 0, place(SRC) < count_of(SRC) - 1
     near_count, far_count = count_of(NEAR), count_of(FAR)
     near_me, far_me = place(NEAR), place(FAR)
+    def tell(semaphore, device):
+        pl.semaphore_signal(semaphore, inc=1, device_id=device, device_id_type=MESH)
+
     barrier = pltpu.get_barrier_semaphore()
-    for flag, device in ((has_before, before), (has_after, after)):
-        @pl.when(flag)
-        def _():
-            pl.semaphore_signal(barrier, inc=1, device_id=device, device_id_type=MESH)
-    for axes, count in ((NEAR, near_count), (FAR, far_count)):
-        @pl.loop(1, count)
-        def _(step):
-            pl.semaphore_signal(barrier, inc=1, device_id=beside(axes, step), device_id_type=MESH)
+    greeted = sum(flag.astype(jnp.int32) for flag in (has_before, has_after, has_lower, has_upper))
+    pl.when(has_lower)(lambda: tell(barrier, lower))
+    pl.when(has_upper)(lambda: tell(barrier, upper))
+    pl.when(has_before)(lambda: tell(barrier, before))
+    pl.when(has_after)(lambda: tell(barrier, after))
+    for ring in RINGS:
+        if count_of(ring) > 1:
+            tell(barrier, beside(ring, -1))
+            tell(barrier, beside(ring, 1))
+            greeted += 2
+
+    def spread_word(turn):
+        for ring in RINGS[:3]:
+            if count_of(ring) > 1:
+                step = 2 if turn and ring == RINGS[2] and count_of(ring) > 4 else 1
+                tell(known.at[turn], beside(ring, -step))
+                tell(known.at[turn], beside(ring, step))
+
+    def hear_word(turn):
+        pl.semaphore_wait(known.at[turn], 2 * sum(count_of(ring) > 1 for ring in RINGS[:3]))
 
     def to_left(f):
         return pltpu.make_async_remote_copy(
             src_ref=xv.at[:, f, pl.ds(0, HALO)], dst_ref=right.at[f],
-            send_sem=send_sem.at[0, f], recv_sem=right_sem.at[f],
+            send_sem=send_sem.at[0], recv_sem=right_sem.at[f],
             device_id=before, device_id_type=MESH)
 
     def to_right(f):
         return pltpu.make_async_remote_copy(
             src_ref=xv.at[:, f, pl.ds(ROWS - HALO, HALO)], dst_ref=left.at[f],
-            send_sem=send_sem.at[1, f], recv_sem=left_sem.at[f],
+            send_sem=send_sem.at[1], recv_sem=left_sem.at[f],
             device_id=after, device_id_type=MESH)
 
     def aux(i, source, target, device):
@@ -132,8 +156,8 @@
 
     masks = ((aux(0, mask_own, mask_right, before), has_before, has_after),
              (aux(1, mask_own, mask_left, after), has_after, has_before))
-    ends = ((aux(2, edges, edges_right, beside(SRC, -1)), has_lower, has_upper),
-            (aux(3, edges, edges_left, beside(SRC, 1)), has_upper, has_lower))
+    ends = ((aux(2, edges, edges_right, lower), has_lower, has_upper),
+            (aux(3, edges, edges_left, upper), has_upper, has_lower))
     rims = ((aux(4, rim.at[pl.ds(0, HALO)], rim_right, before), has_before, has_after),
             (aux(5, rim.at[pl.ds(ROWS - HALO, HALO)], rim_left, after), has_after, has_before))
 
@@ -155,9 +179,7 @@
             def _(f):
                 copy(f).start()
 
-    for g in range(GROUPS):
-        fetch(g).wait()
-    for copy in (mask_copy, taper_copy):
+    for copy in (*fetches, mask_copy, taper_copy):
         copy.wait()
     weights = [taper_ref[i] for i in range(5)]
     shift = shift_ref[0]
@@ -174,13 +196,12 @@
         edges[...] = lax.fori_loop(0, slices, pack, jnp.zeros(edges.shape, jnp.float32), unroll=4)
 
     with jax.named_scope("barrier"):
-        neighbours = has_before.astype(jnp.int32) + has_after.astype(jnp.int32)
-        pl.semaphore_wait(barrier, neighbours + (near_count - 1) + (far_count - 1))
-
+        pl.semaphore_wait(barrier, greeted)
     start(ends)
     start(masks)
     bulk(to_left, has_before, 0, early_left)
     bulk(to_right, has_after, 0, early_right)
+    spread_word(0)
 
     with jax.named_scope("clear"):
         @pl.when(jnp.logical_not(has_before))
@@ -203,6 +224,9 @@
         def _():
             edges_right[...] = jnp.zeros_like(edges_right)
 
+    with jax.named_scope("word0"):
+        hear_word(0)
+        spread_word(1)
     with jax.named_scope("maskwait"):
         arrive(masks)
     lane_half = lanes_of((1, ROWS))
@@ -232,6 +256,9 @@
                     bands[f, base + ROWS:base + 2 * ROWS, :LANES] = imag
                     bands[f, base + ROWS:base + 2 * ROWS, LANES:] = real
 
+    with jax.named_scope("word1"):
+        hear_word(1)
+        spread_word(2)
     with jax.named_scope("edgewait"):
         arrive(ends)
     rim[...] = jnp.where(lax.rem(lanes_of(rim.shape), 4) < 2, edges_left[...], edges_right[...])
@@ -247,7 +274,7 @@
             low[f, pl.ds(c * LANES + first, ROWS), columns] = l
 
     with jax.named_scope("own"):
-        @pl.loop(0, slices)
+        @pl.loop(0, slices, unroll=2)
         def _(f):
             squares = jnp.zeros((1, LANES), jnp.float32)
             for c in range(2):
@@ -257,6 +284,8 @@
                 squares += jnp.sum(x0 * x0 + x1 * x1, axis=0, keepdims=True)
             parts[pl.ds(f, 1), :] = squares
 
+    with jax.named_scope("word2"):
+        hear_word(2)
     with jax.named_scope("rimwait"):
         arrive(rims)
 
@@ -266,11 +295,12 @@
 
     rim_halo = blend(rim_right[...], rim_left[...])
 
-    @pl.loop(0, slices)
-    def _(f):
+    def arrived(f):
         with jax.named_scope("bulkwait"):
             pl.when(has_after)(to_left(f).wait_recv)
             pl.when(has_before)(to_right(f).wait_recv)
+
+    def finish(f):
         for c in range(2):
             h = pltpu.roll(rim_halo, LANES - 2 - 4 * (c * slices + f), 1)
             x = blend(right[f, c], left[f, c])
@@ -283,66 +313,67 @@
         squares = jnp.sum(result * result, axis=0, keepdims=True)
         parts[pl.ds(slices + f, 1), :] = squares[:, :LANES] + squares[:, LANES:]
 
+    @pl.loop(0, slices // 2 - 1)
+    def _(g):
+        for f in (2 * g, 2 * g + 1):
+            arrived(f)
+        for f in (2 * g, 2 * g + 1):
+            finish(f)
+
+    @pl.loop(slices - 2, slices)
+    def _(f):
+        arrived(f)
+        finish(f)
+
     shape = parts.shape
     diagonal = lanes_of(shape) == rows_of(shape)
 
     def to_row(column):
         return jnp.sum(jnp.where(diagonal, column, 0.0), axis=0, keepdims=True)
 
-    def total(axes, me, count, slots, sends, recvs, energy, stage):
+    def total(rings, me, count, slots, sems, energy, stage, between):
         row[stage] = energy
         slots[me] = energy
 
-        def copy(step, slot):
-            return pltpu.make_async_remote_copy(
-                src_ref=row.at[stage], dst_ref=slots.at[slot], send_sem=sends.at[step], recv_sem=recvs.at[slot],
-                device_id=beside(axes, step), device_id_type=MESH)
-
-        @pl.loop(1, count)
-        def _(step):
-            copy(step, me).start()
-
-        @pl.loop(1, count)
-        def _(step):
-            copy(step, lax.rem(me + step, count)).wait_recv()
-
+        for device in others_of(rings):
+            pltpu.make_async_remote_copy(
+                src_ref=row.at[stage], dst_ref=slots.at[me], send_sem=sems.at[0], recv_sem=sems.at[1],
+                device_id=device, device_id_type=MESH).start()
+
+        between()
+        others = slots.at[pl.ds(0, count - 1)]
+        every = pltpu.make_async_remote_copy(
+            src_ref=others, dst_ref=others, send_sem=sems.at[0], recv_sem=sems.at[1],
+            device_id=beside(rings[0], 1), device_id_type=MESH)
+        every.wait_recv()
         result = slots[0]
         for slot in range(1, count):
             result = result + slots[slot]
-        return result
+        return result, every
+
+    def sent():
+        for copy, sends, _ in masks + ends + rims:
+            pl.when(sends)(copy.wait_send)
+        for side, flag, device in ((0, has_before, before), (1, has_after, after)):
+            @pl.when(flag)
+            def _():
+                whole = xv.at[:, :, pl.ds(side * (ROWS - HALO), HALO)]
+                pltpu.make_async_remote_copy(
+                    src_ref=whole, dst_ref=whole, send_sem=send_sem.at[side], recv_sem=send_sem.at[side],
+                    device_id=device, device_id_type=MESH).wait_send()
 
     energy = to_row(jnp.sum(parts[...], axis=1, keepdims=True))
     with jax.named_scope("near"):
-        energy = total(NEAR, near_me, near_count, near, near_send, near_recv, energy, 0)
+        energy, near_all = total(RINGS[2:], near_me, near_count, near, near_sem, energy, 0, sent)
     with jax.named_scope("far"):
-        energy = total(FAR, far_me, far_count, far, far_send, far_recv, energy, 1)
+        energy, far_all = total(RINGS[:2], far_me, far_count, far, far_sem, energy, 1, near_all.wait_send)
     predicted = pltpu.roll(energy, LANES - slices, 1)
     gain = jnp.sqrt((energy + 1e-06) / (predicted + 1e-06))
     spread = jnp.sum(jnp.where(diagonal[:slices], gain, 0.0), axis=1, keepdims=True)
     gain_ref[...] = jnp.broadcast_to(spread, gain_ref.shape)
 
     with jax.named_scope("sendwait"):
-        for copy, sends, _ in masks + ends + rims:
-            pl.when(sends)(copy.wait_send)
-
-        @pl.when(has_before)
-        def _():
-            @pl.loop(0, slices)
-            def _(f):
-                to_left(f).wait_send()
-
-        @pl.when(has_after)
-        def _():
-            @pl.loop(0, slices)
-            def _(f):
-                to_right(f).wait_send()
-
-        for stage, (axes, count, sends) in enumerate(((NEAR, near_count, near_send), (FAR, far_count, far_send))):
-            @pl.loop(1, count)
-            def _(step):
-                pltpu.make_async_remote_copy(
-                    src_ref=row.at[stage], dst_ref=row.at[stage], send_sem=sends.at[step], recv_sem=sends.at[step],
-                    device_id=beside(axes, step), device_id_type=MESH).wait_send()
+        far_all.wait_send()
 
 
 def subtract(x_ref, mult_ref, gain_ref, mult_hbm, prim_hbm, prim, mult_sem, prim_sem):
@@ -408,19 +439,18 @@
             pltpu.VMEM((2, 1, LANES), f32),
             pltpu.VMEM((near_count, 1, LANES), f32),
             pltpu.VMEM((far_count, 1, LANES), f32),
-            dma((GROUPS,)),
+            dma((2,)),
             dma(()),
             dma(()),
             dma(()),
-            dma((2, slices)),
+            dma((2,)),
             dma((slices,)),
             dma((slices,)),
             dma((6,)),
             dma((6,)),
-            dma((near_count,)),
-            dma((near_count,)),
-            dma((far_count,)),
-            dma((far_count,)),
+            dma((2,)),
+            dma((2,)),
+            pltpu.SemaphoreType.REGULAR((3,)),
         ],
         compiler_params=pltpu.CompilerParams(
             collective_id=0, has_side_effects=True, vmem_limit_bytes=40 * 1024 * 1024),

time: 45.3 us -> 42.7 us (0.943)
  Pallas kernels: 43.9 us -> 41.3 us
    pallas_call x1, Pallas kernels: 41.8 us -> 39.2 us  [per_device(): pl.pallas_call(predict, out_shape=(field, field, jax.ShapeDtypeStruct((sl...]
where the time goes in v3:
time: 42.7 us; the launch traced here: 42.6 us
  Pallas kernels  41.3 us (97%)
  between operations  1.28 us (3%)
    pallas_call x1, Pallas kernels, per_device(): pl.pallas_call(predict, out_shape=(field, field, jax.ShapeDtypeStruct((sl...  39.2 us
    pallas_call x1, Pallas kernels, per_device(): pl.pallas_call(subtract, out_shape=(field, field), in_specs=[whole, whole...  2.07 us

profile of v3, /device:TPU:1, one launch (start us, length us, event | category | flops | bytes accessed | tf_op | source)
XLA Modules:
  0.0 42.6 jit_solution(10010511458561131315)
XLA Ops:
  1.3 39.2 %predict.1 = (f32[2,16,64,256]{3,2,1,0:T(8,128)S(1)}, f32[2,16,64,256]{3,2,1,0:T(8,128)S(1)}, f32[16,128]{1,0:T(8,128)S(1)}) custom-call(f32[2,16,64,256]{3,2,1,0:T(8,128)} %x_hbm.1, f32[2,64,1024]{2,1,0:T(8,128)} %band_hbm.1, s32[1]{0:T(128)S(6)} %copy.7.shift_ref, s32[1,64]{1,0:T(1,128)} %bitcast.1, f32[5]{0:T(128)} %taper_hbm.1), custom_call_target="tpu_custom_call" | custom-call | tf_op jit(solution)/shard_map/predict/pallas_call | solution.py:416
  40.5 2.1 %subtract.1 = (f32[2,16,64,256]{3,2,1,0:T(8,128)}, f32[2,16,64,256]{3,2,1,0:T(8,128)}) custom-call(f32[2,16,64,256]{3,2,1,0:T(8,128)S(1)} %get-tuple-element.5.x_ref, f32[2,16,64,256]{3,2,1,0:T(8,128)S(1)} %get-tuple-element.6.mult_ref, f32[16,128]{1,0:T(8,128)S(1)} %get-tuple-element.7.gain_ref), custom_call_target="tpu_custom_call" | custom-call | tf_op jit(solution)/shard_map/subtract/pallas_call | solution.py:459

commit v4 on v3

--- a/solution.py
+++ b/solution.py
@@ -15,8 +15,9 @@
 NEAR = ("rcv_1", "rcv_2")
 FAR = ("src_0", "src_1", "rcv_0")
 RINGS = (("src_0",), ("src_1", "rcv_0"), ("rcv_1",), ("rcv_2",))
-EARLY = 7
-EARLY_FAR = 3
+EARLY = 6
+EARLY_FAR = 2
+RELAYED = 5
 GROUPS = 4
 MESH = pl.DeviceIdType.MESH
 SPLIT_SIZES = (4, 2, 2, 8, 2)
@@ -86,7 +87,7 @@
     x_hbm, band_hbm, shift_ref, mask_hbm, taper_hbm,
     xv, mult_ref, gain_ref,
     taper_ref, bandv, mask_own, mask_left, mask_right, edges, edges_left, edges_right,
-    rim, rim_left, rim_right, left, right, bands, high, low, parts, row, near, far,
+    rim, rim_left, rim_right, left, right, bands, high, low, tips_high, tips_low, fringe, parts, row, near, far,
     x_sem, band_sem, mask_sem, taper_sem, send_sem, left_sem, right_sem, aux_send, aux_recv,
     near_sem, far_sem, known,
 ):
@@ -112,6 +113,13 @@
     has_lower, has_upper = place(SRC) > 0, place(SRC) < count_of(SRC) - 1
     near_count, far_count = count_of(NEAR), count_of(FAR)
     near_me, far_me = place(NEAR), place(FAR)
+    lines = lax.axis_size("rcv_0")
+    direct = slices - RELAYED if lines > 1 else slices
+    at_start, at_end = near_me == 0, near_me == near_count - 1
+    relays_left = jnp.logical_and(at_start, jnp.logical_not(has_before))
+    relays_right = jnp.logical_and(at_end, jnp.logical_not(has_after))
+    next_line = {"rcv_0": 1 - lax.axis_index("rcv_0")}
+
     def tell(semaphore, device):
         pl.semaphore_signal(semaphore, inc=1, device_id=device, device_id_type=MESH)
 
@@ -127,6 +135,11 @@
             tell(barrier, beside(ring, 1))
             greeted += 2
 
+    if lines > 1:
+        pl.when(at_start)(lambda: tell(barrier, beside(NEAR, -1)))
+        pl.when(at_end)(lambda: tell(barrier, beside(NEAR, 1)))
+        greeted += at_start.astype(jnp.int32) + at_end.astype(jnp.int32)
+
     def spread_word(turn):
         for ring in RINGS[:3]:
             if count_of(ring) > 1:
@@ -137,17 +150,27 @@
     def hear_word(turn):
         pl.semaphore_wait(known.at[turn], 2 * sum(count_of(ring) > 1 for ring in RINGS[:3]))
 
-    def to_left(f):
+    def to_left(f, device):
         return pltpu.make_async_remote_copy(
             src_ref=xv.at[:, f, pl.ds(0, HALO)], dst_ref=right.at[f],
             send_sem=send_sem.at[0], recv_sem=right_sem.at[f],
-            device_id=before, device_id_type=MESH)
-
-    def to_right(f):
+            device_id=device, device_id_type=MESH)
+
+    def to_right(f, device):
         return pltpu.make_async_remote_copy(
             src_ref=xv.at[:, f, pl.ds(ROWS - HALO, HALO)], dst_ref=left.at[f],
             send_sem=send_sem.at[1], recv_sem=left_sem.at[f],
-            device_id=after, device_id_type=MESH)
+            device_id=device, device_id_type=MESH)
+
+    def to_relay(f, rows, buffer, sems, side):
+        return pltpu.make_async_remote_copy(
+            src_ref=xv.at[:, f, rows], dst_ref=buffer.at[f], send_sem=send_sem.at[side], recv_sem=sems.at[f],
+            device_id=next_line, device_id_type=MESH)
+
+    def from_relay(f, source, target, sems, step):
+        return pltpu.make_async_remote_copy(
+            src_ref=source.at[f], dst_ref=target.at[f], send_sem=send_sem.at[2], recv_sem=sems.at[f],
+            device_id=beside(NEAR, step), device_id_type=MESH)
 
     def aux(i, source, target, device):
         return pltpu.make_async_remote_copy(
@@ -169,15 +192,15 @@
         for copy, _, receives in entries:
             pl.when(receives)(copy.wait_recv)
 
-    early_left = jnp.where(near_me == 0, EARLY_FAR, EARLY)
-    early_right = jnp.where(near_me == near_count - 1, EARLY_FAR, EARLY)
-
-    def bulk(copy, flag, first, last):
+    early_left, last_left = jnp.where(at_start, EARLY_FAR, EARLY), jnp.where(at_start, direct, slices)
+    early_right, last_right = jnp.where(at_end, EARLY_FAR, EARLY), jnp.where(at_end, direct, slices)
+
+    def bulk(copy, flag, device, first, last):
         @pl.when(flag)
         def _():
             @pl.loop(first, last)
             def _(f):
-                copy(f).start()
+                copy(f, device).start()
 
     for copy in (*fetches, mask_copy, taper_copy):
         copy.wait()
@@ -199,8 +222,17 @@
         pl.semaphore_wait(barrier, greeted)
     start(ends)
     start(masks)
-    bulk(to_left, has_before, 0, early_left)
-    bulk(to_right, has_after, 0, early_right)
+    bulk(to_left, has_before, before, 0, early_left)
+    bulk(to_right, has_after, after, 0, early_right)
+    if lines > 1:
+        for flag, rows, buffer, sems, side in (
+                (jnp.logical_and(at_start, has_before), pl.ds(0, HALO), left, left_sem, 0),
+                (jnp.logical_and(at_end, has_after), pl.ds(ROWS - HALO, HALO), right, right_sem, 1)):
+            @pl.when(flag)
+            def _():
+                @pl.loop(direct, slices)
+                def _(f):
+                    to_relay(f, rows, buffer, sems, side).start()
     spread_word(0)
 
     with jax.named_scope("clear"):
@@ -208,13 +240,13 @@
         def _():
             mask_left[...] = jnp.zeros_like(mask_left)
             rim_left[...] = jnp.zeros_like(rim_left)
-            left[...] = jnp.zeros_like(left)
+            left[pl.ds(0, direct)] = jnp.zeros((direct, *left.shape[1:]), jnp.float32)
 
         @pl.when(jnp.logical_not(has_after))
         def _():
             mask_right[...] = jnp.zeros_like(mask_right)
             rim_right[...] = jnp.zeros_like(rim_right)
-            right[...] = jnp.zeros_like(right)
+            right[pl.ds(0, direct)] = jnp.zeros((direct, *right.shape[1:]), jnp.float32)
 
         @pl.when(jnp.logical_not(has_lower))
         def _():
@@ -223,6 +255,23 @@
         @pl.when(jnp.logical_not(has_upper))
         def _():
             edges_right[...] = jnp.zeros_like(edges_right)
+
+    def put(f, c, first, values):
+        for side, value in enumerate(values):
+            h, l = halves(value)
+            columns = slice(side * LANES, (side + 1) * LANES)
+            high[f, pl.ds(c * LANES + first, ROWS), columns] = h
+            low[f, pl.ds(c * LANES + first, ROWS), columns] = l
+
+    with jax.named_scope("own"):
+        @pl.loop(0, slices, unroll=2)
+        def _(f):
+            squares = jnp.zeros((1, LANES), jnp.float32)
+            for c in range(2):
+                x0, x1 = xv[c, f, :, :LANES], xv[c, f, :, LANES:]
+                put(f, c, 0, (x0, x1))
+                squares += jnp.sum(x0 * x0 + x1 * x1, axis=0, keepdims=True)
+            parts[pl.ds(f, 1), :] = squares
 
     with jax.named_scope("word0"):
         hear_word(0)
@@ -263,26 +312,8 @@
         arrive(ends)
     rim[...] = jnp.where(lax.rem(lanes_of(rim.shape), 4) < 2, edges_left[...], edges_right[...])
     start(rims)
-    bulk(to_left, has_before, early_left, slices)
-    bulk(to_right, has_after, early_right, slices)
-
-    def put(f, c, first, values):
-        for side, value in enumerate(values):
-            h, l = halves(value)
-            columns = slice(side * LANES, (side + 1) * LANES)
-            high[f, pl.ds(c * LANES + first, ROWS), columns] = h
-            low[f, pl.ds(c * LANES + first, ROWS), columns] = l
-
-    with jax.named_scope("own"):
-        @pl.loop(0, slices, unroll=2)
-        def _(f):
-            squares = jnp.zeros((1, LANES), jnp.float32)
-            for c in range(2):
-                h = pltpu.roll(rim[...], LANES - 2 - 4 * (c * slices + f), 1)
-                x0, x1 = xv[c, f, :, :LANES], xv[c, f, :, LANES:]
-                put(f, c, 0, taper(h, x0, x1, weights))
-                squares += jnp.sum(x0 * x0 + x1 * x1, axis=0, keepdims=True)
-            parts[pl.ds(f, 1), :] = squares
+    bulk(to_left, has_before, before, early_left, last_left)
+    bulk(to_right, has_after, after, early_right, last_right)
 
     with jax.named_scope("word2"):
         hear_word(2)
@@ -293,25 +324,48 @@
         rows = rows_of((32, r.shape[1])) + 16
         return jnp.concatenate([r[:16], jnp.where(rows <= 30 + shift, r[16:], l[:32]), l[32:]], axis=0)
 
-    rim_halo = blend(rim_right[...], rim_left[...])
+    if lines > 1:
+        with jax.named_scope("relay"):
+            for flag, source, came, target, sems, step in (
+                    (relays_left, left, left_sem, right, right_sem, -1),
+                    (relays_right, right, right_sem, left, left_sem, 1)):
+                @pl.when(flag)
+                def _():
+                    @pl.loop(direct, slices)
+                    def _(f):
+                        from_relay(f, source, source, came, step).wait_recv()
+                        from_relay(f, source, target, sems, step).start()
+
+    tips = jnp.concatenate([rim[...], blend(rim_right[...], rim_left[...])], axis=0)
+    tips_high[...], tips_low[...] = halves(jnp.concatenate([tips, pltpu.roll(tips, LANES // 2, 1)], axis=0))
+
+    def product(f, x_high, x_low):
+        wide = jnp.dot(bands[f], x_high, preferred_element_type=jnp.float32)
+        thin = jnp.dot(bands[f, :LANES], x_low, preferred_element_type=jnp.float32)
+        return wide[:LANES] + wide[LANES:] + thin
+
+    with jax.named_scope("fringe"):
+        @pl.loop(0, slices, unroll=2)
+        def _(f):
+            fringe[f] = pltpu.roll(product(f, tips_high[...], tips_low[...]), LANES - 2 - 4 * f, 1)
 
     def arrived(f):
         with jax.named_scope("bulkwait"):
-            pl.when(has_after)(to_left(f).wait_recv)
-            pl.when(has_before)(to_right(f).wait_recv)
+            pl.when(has_after)(to_left(f, before).wait_recv)
+            pl.when(has_before)(to_right(f, after).wait_recv)
 
     def finish(f):
         for c in range(2):
-            h = pltpu.roll(rim_halo, LANES - 2 - 4 * (c * slices + f), 1)
             x = blend(right[f, c], left[f, c])
-            put(f, c, ROWS, taper(h, x[:, :LANES], x[:, LANES:], weights))
-        wide = jnp.dot(bands[f], high[f], preferred_element_type=jnp.float32)
-        thin = jnp.dot(bands[f, :LANES], low[f], preferred_element_type=jnp.float32)
-        result = wide[:LANES] + wide[LANES:] + thin
-        mult_ref[0, f] = result[:ROWS]
-        mult_ref[1, f] = result[ROWS:]
-        squares = jnp.sum(result * result, axis=0, keepdims=True)
-        parts[pl.ds(slices + f, 1), :] = squares[:, :LANES] + squares[:, LANES:]
+            put(f, c, ROWS, (x[:, :LANES], x[:, LANES:]))
+        predicted = product(f, high[f], low[f])
+        squares = jnp.zeros((1, LANES), jnp.float32)
+        for side, value in enumerate(taper(fringe[f], predicted[:, :LANES], predicted[:, LANES:], weights)):
+            columns = slice(side * LANES, (side + 1) * LANES)
+            mult_ref[0, f, :, columns] = value[:ROWS]
+            mult_ref[1, f, :, columns] = value[ROWS:]
+            squares += jnp.sum(value * value, axis=0, keepdims=True)
+        parts[pl.ds(slices + f, 1), :] = squares
 
     @pl.loop(0, slices // 2 - 1)
     def _(g):
@@ -361,6 +415,15 @@
                 pltpu.make_async_remote_copy(
                     src_ref=whole, dst_ref=whole, send_sem=send_sem.at[side], recv_sem=send_sem.at[side],
                     device_id=device, device_id_type=MESH).wait_send()
+
+        if lines > 1:
+            for flag, buffer in ((relays_left, left), (relays_right, right)):
+                @pl.when(flag)
+                def _():
+                    whole = buffer.at[pl.ds(direct, RELAYED)]
+                    pltpu.make_async_remote_copy(
+                        src_ref=whole, dst_ref=whole, send_sem=send_sem.at[2], recv_sem=send_sem.at[2],
+                        device_id=next_line, device_id_type=MESH).wait_send()
 
     energy = to_row(jnp.sum(parts[...], axis=1, keepdims=True))
     with jax.named_scope("near"):
@@ -435,6 +498,9 @@
             pltpu.VMEM((slices, 4 * receivers, 2 * LANES), bf16),
             pltpu.VMEM((slices, 2 * LANES, shots), bf16),
             pltpu.VMEM((slices, 2 * LANES, shots), bf16),
+            pltpu.VMEM((4 * receivers, LANES), bf16),
+            pltpu.VMEM((4 * receivers, LANES), bf16),
+            pltpu.VMEM((slices, 2 * receivers, LANES), f32),
             pltpu.VMEM((2 * slices, LANES), f32),
             pltpu.VMEM((2, 1, LANES), f32),
             pltpu.VMEM((near_count, 1, LANES), f32),
@@ -443,7 +509,7 @@
             dma(()),
             dma(()),
             dma(()),
-            dma((2,)),
+            dma((3,)),
             dma((slices,)),
             dma((slices,)),
             dma((6,)),

time: 42.7 us -> 42.1 us (0.986)
  Pallas kernels: 41.3 us -> 40.7 us
    pallas_call x1, Pallas kernels: 39.2 us -> 38.6 us  [per_device(): pl.pallas_call(predict, out_shape=(field, field, jax.ShapeDtypeStruct((sl...]
where the time goes in v4:
time: 42.1 us; the launch traced here: 42 us
  Pallas kernels  40.7 us (97%)
  between operations  1.28 us (3%)
    pallas_call x1, Pallas kernels, per_device(): pl.pallas_call(predict, out_shape=(field, field, jax.ShapeDtypeStruct((sl...  38.6 us
    pallas_call x1, Pallas kernels, per_device(): pl.pallas_call(subtract, out_shape=(field, field), in_specs=[whole, whole...  2.07 us

profile of v4, /device:TPU:1, one launch (start us, length us, event | category | flops | bytes accessed | tf_op | source)
XLA Modules:
  0.0 42.0 jit_solution(6531886847070324936)
XLA Ops:
  1.3 38.6 %predict.1 = (f32[2,16,64,256]{3,2,1,0:T(8,128)S(1)}, f32[2,16,64,256]{3,2,1,0:T(8,128)S(1)}, f32[16,128]{1,0:T(8,128)S(1)}) custom-call(f32[2,16,64,256]{3,2,1,0:T(8,128)} %x_hbm.1, f32[2,64,1024]{2,1,0:T(8,128)} %band_hbm.1, s32[1]{0:T(128)S(6)} %copy.7.shift_ref, s32[1,64]{1,0:T(1,128)} %bitcast.1, f32[5]{0:T(128)} %taper_hbm.1), custom_call_target="tpu_custom_call" | custom-call | tf_op jit(solution)/shard_map/predict/pallas_call | solution.py:479
  39.9 2.1 %subtract.1 = (f32[2,16,64,256]{3,2,1,0:T(8,128)}, f32[2,16,64,256]{3,2,1,0:T(8,128)}) custom-call(f32[2,16,64,256]{3,2,1,0:T(8,128)S(1)} %get-tuple-element.5.x_ref, f32[2,16,64,256]{3,2,1,0:T(8,128)S(1)} %get-tuple-element.6.mult_ref, f32[16,128]{1,0:T(8,128)S(1)} %get-tuple-element.7.gain_ref), custom_call_target="tpu_custom_call" | custom-call | tf_op jit(solution)/shard_map/subtract/pallas_call | solution.py:525
